TPU v7x, 32 devices: a whole 2x2x4 slice. The times are simulated.
32 devices in a mesh: dp: 1, tp: 32 (over x, y, z, core).
Axes of the slice: x: 2, y: 2, z: 4, core: 2. Of those that a mesh axis runs over, the one named last changes fastest.
Arguments:
- x: bfloat16 [2048, 5120], P('dp')
- dy: bfloat16 [2048, 5120], P('dp')
- gate: bfloat16 [2048, 32768], P('dp', 'tp')
- up: bfloat16 [2048, 32768], P('dp', 'tp')
- w_gate: bfloat16 [5120, 32768], P(None, 'tp')
- w_up: bfloat16 [5120, 32768], P(None, 'tp')
- w_down: bfloat16 [32768, 5120], P('tp')
Outputs:
- output 1: bfloat16 [2048, 5120], P('dp')
- output 2: bfloat16 [5120, 32768], P('dp', 'tp')
- output 3: bfloat16 [5120, 32768], P('dp', 'tp')
- output 4: bfloat16 [32768, 5120], P(('dp', 'tp'))
All inputs are finite; a program needn't handle non-finite values.
Results may differ from a plain program's by a relative error of at most 0.012.
Values are sent between devices in bfloat16 or wider.
A program may use at most 2 GiB of HBM per device.

v0:
```python
import jax
import jax.numpy as jnp
from jax import lax
from jax.sharding import PartitionSpec as P


def act(gate, up):
    return jax.nn.silu(gate) * up


def solution(mesh):
    def step(x, dy, gate, up, w_gate, w_up, w_down):
        hidden, back = jax.vjp(act, gate.astype(jnp.float32), up.astype(jnp.float32))
        d_hidden = jnp.dot(dy, w_down.T, preferred_element_type=jnp.float32)
        d_gate, d_up = (g.astype(jnp.bfloat16) for g in back(d_hidden))
        term = jnp.dot(d_gate, w_gate.T, preferred_element_type=jnp.float32) + jnp.dot(d_up, w_up.T, preferred_element_type=jnp.float32)
        dx = lax.psum(term.astype(jnp.bfloat16), "tp")
        dw_gate = jnp.dot(x.T, d_gate, preferred_element_type=jnp.float32)
        dw_up = jnp.dot(x.T, d_up, preferred_element_type=jnp.float32)
        dw_down = jnp.dot(hidden.astype(jnp.bfloat16).T, dy, preferred_element_type=jnp.float32)
        return dx, *(g.astype(jnp.bfloat16) for g in (dw_gate, dw_up, dw_down))

    tokens, columns, rows = P("dp", None), P(None, "tp"), P("tp", None)
    return jax.shard_map(
        step,
        mesh=mesh,
        in_specs=(tokens, tokens, P("dp", "tp"), P("dp", "tp"), columns, columns, rows),
        out_specs=(tokens, P("dp", "tp"), P("dp", "tp"), P(("dp", "tp"), None)),
        check_vma=False,
    )
```

profile of v0, /device:TPU:0, one launch (start us, length us, event | category | flops | bytes accessed | tf_op | source)
XLA Modules:
  0.0 462.4 jit_solution(14909935687843092483)
XLA Ops:
  7.2 0.0 all-reduce.2.cloned.1.call-start
  7.2 32.8 %fusion.6 = (bf16[2048,1024]{1,0:T(8,128)(2,1)}, f32[2048,1024]{1,0:T(8,128)}) fusion(bf16[2048,1024]{1,0:T(8,128)(2,1)} %param.9, bf16[2048,1024]{1,0:T(8,128)(2,1)} %param.10, bf16[2048,5120]{1,0:T(8,128)(2,1)} %param.8, bf16[1024,5120]{1,0:T(8,128)(2,1)} %param.13), kind=kOutput, calls=%fused_computation.16 | convolution fusion | flops 21502099456 | bytes 52428800 | tf_op jit(solution)/shard_map/dot_general | solution.py:14
  40.0 29.6 %fusion.9 = f32[2048,5120]{1,0:T(8,128)} fusion(bf16[2048,1024]{1,0:T(8,128)(2,1)} %get-tuple-element.8, bf16[5120,1024]{1,0:T(8,128)(2,1)} %param.11), kind=kOutput, calls=%fused_computation.19 | convolution fusion | flops 21474836480 | bytes 56623104 | tf_op jit(solution)/shard_map/dot_general | solution.py:16
  69.6 36.8 %add_convert_fusion = bf16[2048,5120]{1,0:T(8,128)(2,1)} fusion(f32[2048,5120]{1,0:T(8,128)} %fusion.9, bf16[5120,1024]{1,0:T(8,128)(2,1)} %param.12, f32[2048,1024]{1,0:T(8,128)} %get-tuple-element.9, bf16[2048,1024]{1,0:T(8,128)(2,1)} %param.9), kind=kOutput, calls=%fused_computation | convolution fusion | flops 21510488064 | bytes 85983232 | tf_op jit(solution)/shard_map/dot_general | solution.py:16
  106.4 0.0 all-reduce.2.cloned.1.call-update
  106.4 28.3 %convert_bitcast_fusion.1 = bf16[5120,1024]{0,1:T(8,128)(2,1)} fusion(bf16[2048,1024]{1,0:T(8,128)(2,1)} %get-tuple-element.8, bf16[2048,5120]{1,0:T(8,128)(2,1)} %param.7), kind=kOutput, calls=%fused_computation.8 | convolution fusion | flops 21480079360 | bytes 35651584 | tf_op jit(solution)/shard_map/dot_general | solution.py:18
  134.7 14.4 %copy.11 = bf16[5120,1024]{1,0:T(8,128)(2,1)} copy(bf16[5120,1024]{0,1:T(8,128)(2,1)} %convert_bitcast_fusion.1) | data formatting | bytes 20971520
  149.1 33.9 %convert_bitcast_fusion = bf16[5120,1024]{0,1:T(8,128)(2,1)} fusion(bf16[2048,5120]{1,0:T(8,128)(2,1)} %param.7, f32[2048,1024]{1,0:T(8,128)} %get-tuple-element.9, bf16[2048,1024]{1,0:T(8,128)(2,1)} %param.9), kind=kOutput, calls=%fused_computation.7 | convolution fusion | flops 21494759424 | bytes 44040192 | tf_op jit(solution)/shard_map/dot_general | solution.py:19
  182.9 14.4 %copy.12 = bf16[5120,1024]{1,0:T(8,128)(2,1)} copy(bf16[5120,1024]{0,1:T(8,128)(2,1)} %convert_bitcast_fusion) | data formatting | bytes 20971520
  197.3 33.2 %convolution_convert_fusion = bf16[1024,5120]{1,0:T(8,128)(2,1)} fusion(bf16[2048,5120]{1,0:T(8,128)(2,1)} %param.8, bf16[2048,1024]{1,0:T(8,128)(2,1)} %param.10, bf16[2048,1024]{1,0:T(8,128)(2,1)} %param.9), kind=kOutput, calls=%fused_computation.9 | convolution fusion | flops 21496856576 | bytes 39845888 | tf_op jit(solution)/shard_map/dot_general | solution.py:20
  230.6 207.7 %all-reduce.2.cloned.1.call-done = bf16[2048,5120]{1,0:T(8,128)(2,1)} async-done(((bf16[2048,5120]{1,0:T(8,128)(2,1)}), bf16[2048,5120]{1,0:T(8,128)(2,1)}) %all-reduce.2.cloned.1.call-update) | async-done | bytes 20971536 | tf_op jit(solution)/shard_map/psum | solution.py:17
  438.3 17.3 %copy.14 = bf16[2048,5120]{1,0:T(8,128)(2,1)} copy(bf16[2048,5120]{1,0:T(8,128)(2,1)} %all-reduce.2.cloned.1.call-done) | data formatting | bytes 41943040
Async XLA Ops:
  7.2 431.1 %all-reduce.2.cloned.1.call-start = ((), (), s32[]{:S(2)}) async-start(), calls=%async_computation | async-start | bytes 41943040 | tf_op jit(solution)/shard_map/psum | solution.py:17
Sparse Core Ops, SparseCore 0:
  106.5 331.7 all-reduce.1
where the time goes:
time: 463 us; the launch traced here: 462 us
  waiting for transfers between devices  208 us (45%)
  matrix products  195 us (42%)
  local copies, waits for them, and re-layouts  46.1 us (10%)
  between operations  14 us (3%)
    psum x1, waiting for transfers between devices, step(): dx = lax.psum(term.astype(jnp.bfloat16), 'tp')  208 us
    unnamed x3, local copies, waits for them, and re-layouts  46.1 us
    dot_general x1, matrix products, step(): jnp.dot(d_up, w_up.T, preferred_element_type=jnp.float32)  36.8 us
    dot_general x1, matrix products, step(): dw_up = jnp.dot(x.T, d_up, preferred_element_type=jnp.float32)  33.9 us
    dot_general x1, matrix products, step(): jnp.dot(hidden.astype(jnp.bfloat16).T, dy, preferred_element_type=jnp.flo...  33.2 us
    dot_general x1, matrix products, step(): d_hidden = jnp.dot(dy, w_down.T, preferred_element_type=jnp.float32)  32.8 us
    dot_general x1, matrix products, step(): jnp.dot(d_gate, w_gate.T, preferred_element_type=jnp.float32)  29.6 us
    dot_general x1, matrix products, step(): dw_gate = jnp.dot(x.T, d_gate, preferred_element_type=jnp.float32)  28.3 us
  transfers between devices with their start and end apart: 1, of which 1 were waited for; matrix products, arithmetic and copies ran while one was open for 27% of the time, Pallas kernels for 0%

commit v1 on v0

v1 whole, which is shorter than its diff:
```python
import jax
import jax.numpy as jnp
from jax import lax
from jax.experimental import pallas as pl
from jax.experimental.pallas import tpu as pltpu
from jax.sharding import PartitionSpec as P

N = 2048
D = 5120
F = 1024
R = 256
CH = N // R
H, Q, E = R // 2, R // 4, R // 8
TB = 512
NB = D // TB
BF = jnp.bfloat16
F32 = jnp.float32
COMM = True
WHEN = {"p1": (1, 0), "fold": (2, 1), "mid": (4, 1), "p3": (5, 2), "fin": (6, 2), "unf": (7, 2), "ap1": (9, 2), "acore": (11, 0)}
NTYPE = ("core", "p1", "fold", "mid", "p3", "amid", "unf", "ap1", "acore")


def tb_dot(a, b):
    return lax.dot_general(a, b, (((1,), (1,)), ((), ())), preferred_element_type=F32)


def ta_dot(a, b):
    return lax.dot_general(a, b, (((0,), (0,)), ((), ())), preferred_element_type=F32)


def kernel(dy, gate, up, wg, wu, wd, x,
           dx, dwg, dwu, dwd, dgo, duo, hio,
           wdv, wgv, wuv, dyb, gb, ub, dgb, dub, hib,
           own, sb0, sb1, k1, sbf, sbm, k2, sp3, fin,
           lc, lp, lf, lm, l3,
           insem, wsem, osem, bsem, bout, finsem, ss, rs, cred):
    me = lax.axis_index("tp")
    core = lax.rem(me, 2)
    z = lax.rem(me // 2, 4)
    yy = lax.rem(me // 8, 2)
    xx = me // 16
    c0 = core == 0
    inner = jnp.logical_or(z == 1, z == 2)
    outer = jnp.logical_not(inner)
    peer = me + 1 - 2 * core
    xp = me + 16 - 32 * xx
    yp = me + 8 - 16 * yy
    bit1 = jnp.where(c0, xx, yy)
    d1 = jnp.where(c0, xp, yp)
    d3 = jnp.where(c0, yp, xp)
    dz = jnp.where(lax.rem(z, 2) == 0, me + 2, me - 2)
    dm = jnp.where(z == 1, me + 2, me - 2)
    kc = core * H
    kp = bit1 * Q
    sp = (1 - bit1) * Q
    km = jnp.where(z == 2, E, 0)
    sm = E - km
    T = {n: i for i, n in enumerate(NTYPE)}

    def rd(n, c, src, dst, dev):
        return pltpu.make_async_remote_copy(
            src_ref=src, dst_ref=dst, send_sem=ss.at[T[n], c], recv_sem=rs.at[T[n], c],
            device_id={"tp": dev}, device_id_type=pl.DeviceIdType.MESH)

    def rows(c, off, n):
        return dx.at[pl.ds(pl.multiple_of(c * R + off, 16), n)]

    def cp_core(c):
        return rd("core", c, sb0, lc.at[lax.rem(c, 2)], peer)

    def cp_p1(c):
        return rd("p1", c, sb1.at[lax.rem(c, 2)], lp.at[lax.rem(c, 3)], d1)

    def cp_fold(c):
        return rd("fold", c, sbf.at[lax.rem(c, 2)], lf.at[lax.rem(c, 3)], dz)

    def cp_mid(c):
        return rd("mid", c, sbm.at[lax.rem(c, 2)], lm.at[lax.rem(c, 2)], dm)

    def cp_p3(c):
        return rd("p3", c, sp3.at[lax.rem(c, 2)], l3.at[lax.rem(c, 2)], d3)

    def cp_amid(c):
        return rd("amid", c, fin.at[lax.rem(c, 2)], rows(c, kc + kp + km, E), dm)

    def cp_fin(c):
        s = lax.rem(c, 2)
        return pltpu.make_async_copy(fin.at[s], rows(c, kc + kp + km, E), finsem.at[s])

    def cp_unf(c):
        return rd("unf", c, rows(c, kc + kp, Q), rows(c, kc + kp, Q), dz)

    def cp_ap1(c):
        return rd("ap1", c, rows(c, kc + kp, Q), rows(c, kc + kp, Q), d1)

    def cp_acore(c):
        return rd("acore", c, rows(c, kc, H), rows(c, kc, H), peer)

    def credit(i, dev):
        pl.semaphore_signal(cred.at[i], inc=1, device_id={"tp": dev}, device_id_type=pl.DeviceIdType.MESH)

    CB = 640

    def cols(f):
        @pl.loop(0, D // CB)
        def _(j):
            f(pl.ds(pl.multiple_of(j * CB, 128), CB))

    def ds_(o, n):
        return pl.ds(pl.multiple_of(o, 16), n)

    def e_send_core(c):
        @pl.when(c >= 2)
        def _():
            pl.semaphore_wait(cred.at[0], 1)
        cp_core(c).start()

    def e_p1(c):
        cp = cp_core(c)
        cp.wait_send()
        cp.wait_recv()
        s, t, u = lax.rem(c, 2), lax.rem(c, 4), lax.rem(c, 2)

        @pl.when(c >= 2)
        def _():
            cp_p1(c - 2).wait_send()

        @pl.when(c >= 3)
        def _():
            pl.semaphore_wait(cred.at[1], 1)

        def f(cs):
            sb1[s, :, cs] = (own[ds_(sp, Q), cs] + lc[u, ds_(sp, Q), cs].astype(F32)).astype(BF)
        cols(f)
        cp_p1(c).start()

        def g(cs):
            k1[t, :, cs] = own[ds_(kp, Q), cs] + lc[u, ds_(kp, Q), cs].astype(F32)
        cols(g)

        @pl.when(c < CH - 2)
        def _():
            credit(0, peer)

    def e_fold(c):
        cp_p1(c).wait_recv()
        t, u, s = lax.rem(c, 4), lax.rem(c, 3), lax.rem(c, 2)

        @pl.when(outer)
        def _():
            @pl.when(c >= 2)
            def _():
                cp_fold(c - 2).wait_send()

            @pl.when(c >= 3)
            def _():
                pl.semaphore_wait(cred.at[2], 1)

            def f(cs):
                sbf[s, :, cs] = (k1[t, :, cs] + lp[u, :, cs].astype(F32)).astype(BF)
            cols(f)
            cp_fold(c).start()

        @pl.when(inner)
        def _():
            def f(cs):
                k1[t, :, cs] = k1[t, :, cs] + lp[u, :, cs].astype(F32)
            cols(f)

        @pl.when(c < CH - 3)
        def _():
            credit(1, d1)

    def e_mid(c):
        @pl.when(inner)
        def _():
            cp_fold(c).wait_recv()
            t, u, s = lax.rem(c, 4), lax.rem(c, 3), lax.rem(c, 2)

            @pl.when(c >= 2)
            def _():
                cp_mid(c - 2).wait_send()
                pl.semaphore_wait(cred.at[3], 1)

            def f(cs):
                sbm[s, :, cs] = (k1[t, ds_(sm, E), cs] + lf[u, ds_(sm, E), cs].astype(F32)).astype(BF)
            cols(f)
            cp_mid(c).start()

            def g(cs):
                k2[s, :, cs] = k1[t, ds_(km, E), cs] + lf[u, ds_(km, E), cs].astype(F32)
            cols(g)

            @pl.when(c < CH - 3)
            def _():
                credit(2, dz)

    def e_p3(c):
        @pl.when(inner)
        def _():
            cp_mid(c).wait_recv()
            s = lax.rem(c, 2)

            @pl.when(c >= 2)
            def _():
                cp_p3(c - 2).wait_send()
                pl.semaphore_wait(cred.at[4], 1)

            def f(cs):
                sp3[s, :, cs] = (k2[s, :, cs] + lm[s, :, cs].astype(F32)).astype(BF)
            cols(f)
            cp_p3(c).start()

            @pl.when(c < CH - 2)
            def _():
                credit(3, dm)

    def e_fin(c):
        @pl.when(inner)
        def _():
            cp_p3(c).wait_recv()
            s = lax.rem(c, 2)

            @pl.when(c >= 2)
            def _():
                cp_amid(c - 2).wait_send()

            def f(cs):
                fin[s, :, cs] = (sp3[s, :, cs].astype(F32) + l3[s, :, cs].astype(F32)).astype(BF)
            cols(f)
            cp_amid(c).start()
            cp_fin(c).start()

            @pl.when(c < CH - 2)
            def _():
                credit(4, d3)

    def e_unf(c):
        @pl.when(inner)
        def _():
            cp_fin(c).wait()
            cp_amid(c).wait_recv()
            cp_unf(c).start()
            cp_ap1(c).start()

    def e_ap1(c):
        @pl.when(outer)
        def _():
            cp_unf(c).wait_recv()
            cp_ap1(c).start()

    def e_acore(c):
        cp_ap1(c).wait_recv()
        cp_acore(c).start()

    EV = {"p1": e_p1, "fold": e_fold, "mid": e_mid, "p3": e_p3, "fin": e_fin, "unf": e_unf, "ap1": e_ap1, "acore": e_acore}

    def events(t, pos, lo, hi):
        if not COMM:
            return
        for n, (dt, ps) in WHEN.items():
            if ps != pos or hi - 1 - dt < 0 or lo - dt >= CH:
                continue
            c = t - dt

            @pl.when(jnp.logical_and(c >= 0, c < CH))
            def _(n=n, c=c):
                EV[n](c)

    if COMM:
        bar = pltpu.get_barrier_semaphore()
        for dev in (peer, d1, d3, dz):
            pl.semaphore_signal(bar, inc=1, device_id={"tp": dev}, device_id_type=pl.DeviceIdType.MESH)

        @pl.when(inner)
        def _():
            pl.semaphore_signal(bar, inc=1, device_id={"tp": dm}, device_id_type=pl.DeviceIdType.MESH)

    def ld_dy(i):
        return pltpu.make_async_copy(dy.at[pl.ds(pl.multiple_of(i * R, R), R)], dyb, insem.at[0])

    def ld_g(i):
        return pltpu.make_async_copy(gate.at[pl.ds(pl.multiple_of(i * R, R), R)], gb, insem.at[1])

    def ld_u(i):
        return pltpu.make_async_copy(up.at[pl.ds(pl.multiple_of(i * R, R), R)], ub, insem.at[2])

    def st(i, k):
        src, dst = ((dgb, dgo), (dub, duo), (hib, hio))[k]
        return pltpu.make_async_copy(src, dst.at[pl.ds(pl.multiple_of(i * R, R), R)], osem.at[k])

    lw = [pltpu.make_async_copy(wd, wdv, wsem.at[0]), pltpu.make_async_copy(wg, wgv, wsem.at[1]), pltpu.make_async_copy(wu, wuv, wsem.at[2])]
    ld_dy(0).start()
    lw[0].start()
    ld_g(0).start()
    ld_u(0).start()
    lw[1].start()
    lw[2].start()
    if COMM:
        @pl.when(inner)
        def _():
            pl.semaphore_wait(bar, 5)

        @pl.when(outer)
        def _():
            pl.semaphore_wait(bar, 4)

    def phase_a(i, _):
        @pl.when(i > 0)
        def _():
            for k in range(3):
                st(i - 1, k).wait()

        @pl.when(i == 0)
        def _():
            lw[0].wait()
        ld_dy(i).wait()
        ld_g(i).wait()
        ld_u(i).wait()

        @pl.loop(0, F // 512)
        def _(j):
            cs = pl.ds(pl.multiple_of(j * 512, 512), 512)
            dh = tb_dot(dyb[...], wdv[cs, :])
            g = gb[:, cs].astype(F32)
            u = ub[:, cs].astype(F32)
            s = 1.0 / (1.0 + jnp.exp(-g))
            gs = g * s
            dgb[:, cs] = (dh * u * (s + gs * (1.0 - s))).astype(BF)
            dub[:, cs] = (dh * gs).astype(BF)
            hib[:, cs] = (gs * u).astype(BF)

        for k in range(3):
            st(i, k).start()

        @pl.when(i < CH - 1)
        def _():
            ld_dy(i + 1).start()
            ld_g(i + 1).start()
            ld_u(i + 1).start()

        @pl.when(i == 0)
        def _():
            lw[1].wait()
            lw[2].wait()
        events(i, 0, 0, CH)

        def tblock(j):
            rs_ = pl.ds(pl.multiple_of(j * 512, 512), 512)
            t = tb_dot(dgb[...], wgv[rs_, :]) + tb_dot(dub[...], wuv[rs_, :])
            a, b = t[:H], t[H:]
            own[:, rs_] = jnp.where(c0, a, b)
            sb0[:, rs_] = jnp.where(c0, b, a).astype(BF)

        pl.loop(0, 5)(tblock)
        events(i, 1, 0, CH)
        pl.loop(5, 10)(tblock)
        if COMM:
            e_send_core(i)
        events(i, 2, 0, CH)
        return 0

    lax.fori_loop(0, CH, phase_a, 0)
    for k in range(3):
        st(CH - 1, k).wait()

    dgv, duv = wgv.at[pl.ds(0, N)], wgv.at[pl.ds(N, N)]
    hiv = wuv.at[pl.ds(0, N)]
    K2 = N // 2

    def ld_x(b):
        s = lax.rem(b, 2)
        return pltpu.make_async_copy(x.at[:, pl.ds(pl.multiple_of(b * TB, TB), TB)],
                                     wuv.at[pl.ds(N, N), pl.ds(pl.multiple_of(s * TB, TB), TB)], bsem.at[0, s])

    def ld_dyc(b, h):
        s = lax.rem(b, 2)
        return pltpu.make_async_copy(dy.at[pl.ds(h * K2, K2), pl.ds(pl.multiple_of(b * TB, TB), TB)],
                                     wdv.at[:, pl.ds(pl.multiple_of(s * 2 * TB, TB) + h * TB, TB)], bsem.at[1 + h, s])

    def out_g(b, k):
        s = lax.rem(b, 2)
        v = (wgv, wuv)[k]
        return pltpu.make_async_copy(v.at[pl.ds(pl.multiple_of(2 * N + s * TB, TB), TB)],
                                     (dwg, dwu)[k].at[pl.ds(pl.multiple_of(b * TB, TB), TB)], bout.at[k, s])

    def out_d(b):
        s = lax.rem(b, 2)
        return pltpu.make_async_copy(wdv.at[:, pl.ds(pl.multiple_of(4096 + s * TB, TB), TB)],
                                     dwd.at[:, pl.ds(pl.multiple_of(b * TB, TB), TB)], bout.at[2, s])

    lb = [pltpu.make_async_copy(dgo, dgv, wsem.at[0]), pltpu.make_async_copy(duo, duv, wsem.at[1]), pltpu.make_async_copy(hio, hiv, wsem.at[2])]
    lb[0].start()
    ld_x(0).start()
    lb[1].start()
    lb[2].start()
    ld_dyc(0, 0).start()
    ld_dyc(0, 1).start()

    def phase_b(b, _):
        t = b + CH
        s = lax.rem(b, 2)

        @pl.when(b < NB - 1)
        def _():
            ld_x(b + 1).start()
            ld_dyc(b + 1, 0).start()
            ld_dyc(b + 1, 1).start()

        @pl.when(b == 0)
        def _():
            lb[0].wait()
        ld_x(b).wait()
        xs = pl.ds(pl.multiple_of(s * TB, TB), TB)
        for k in range(2):
            @pl.when(b >= 2)
            def _():
                out_g(b - 2, k).wait()

            if k == 1:
                @pl.when(b == 0)
                def _():
                    lb[1].wait()
            r = ta_dot(wuv[pl.ds(N, N), xs], (dgv, duv)[k][...])
            (wgv, wuv)[k][pl.ds(pl.multiple_of(2 * N + s * TB, TB), TB), :] = r.astype(BF)
            out_g(b, k).start()
            events(t, k, CH, CH + NB)

        @pl.when(b >= 2)
        def _():
            out_d(b - 2).wait()

        @pl.when(b == 0)
        def _():
            lb[2].wait()
        ld_dyc(b, 0).wait()
        ld_dyc(b, 1).wait()
        y0 = wdv[:, pl.ds(pl.multiple_of(s * 2 * TB, TB), TB)]
        y1 = wdv[:, pl.ds(pl.multiple_of(s * 2 * TB, TB) + TB, TB)]
        r = ta_dot(hiv[pl.ds(0, K2), :], y0) + ta_dot(hiv[pl.ds(K2, K2), :], y1)
        wdv[:, pl.ds(pl.multiple_of(4096 + s * TB, TB), TB)] = r.astype(BF)
        out_d(b).start()
        events(t, 2, CH, CH + NB)
        return 0

    lax.fori_loop(0, NB, phase_b, 0)
    last = CH + max(dt for dt, _ in WHEN.values())
    if COMM and last > CH + NB:
        def drain(t, _):
            for p in range(3):
                events(t, p, CH + NB, last)
            return 0
        lax.fori_loop(CH + NB, last, drain, 0)

    for b in (NB - 2, NB - 1):
        out_g(b, 0).wait()
        out_g(b, 1).wait()
        out_d(b).wait()
    if COMM:
        def tail(c, _):
            cp_acore(c).wait_recv()
            cp_acore(c).wait_send()
            cp_ap1(c).wait_send()

            @pl.when(inner)
            def _():
                cp_unf(c).wait_send()
            return 0
        lax.fori_loop(0, CH, tail, 0)
        for c in (CH - 2, CH - 1):
            cp_p1(c).wait_send()

            @pl.when(inner)
            def _():
                cp_mid(c).wait_send()
                cp_p3(c).wait_send()
                cp_amid(c).wait_send()

            @pl.when(outer)
            def _():
                cp_fold(c).wait_send()


def call(dy, gate, up, wg, wu, wd, x):
    s = jax.ShapeDtypeStruct
    V = pltpu.VMEM
    S = pltpu.SemaphoreType
    any_ = pl.BlockSpec(memory_space=pl.ANY)
    return pl.pallas_call(
        kernel,
        in_specs=[any_] * 7,
        out_specs=[any_] * 7,
        out_shape=[s((N, D), BF), s((D, F), BF), s((D, F), BF), s((F, D), BF), s((N, F), BF), s((N, F), BF), s((N, F), BF)],
        scratch_shapes=[
            V((F, D), BF), V((D, F), BF), V((D, F), BF), V((R, D), BF), V((R, F), BF), V((R, F), BF),
            V((R, F), BF), V((R, F), BF), V((R, F), BF),
            V((H, D), F32), V((H, D), BF), V((2, Q, D), BF), V((4, Q, D), F32), V((2, Q, D), BF), V((2, E, D), BF),
            V((2, E, D), F32), V((2, E, D), BF), V((2, E, D), BF),
            V((2, H, D), BF), V((3, Q, D), BF), V((3, Q, D), BF), V((2, E, D), BF), V((2, E, D), BF),
            S.DMA((3,)), S.DMA((3,)), S.DMA((3,)), S.DMA((3, 2)), S.DMA((3, 2)), S.DMA((2,)),
            S.DMA((len(NTYPE), CH)), S.DMA((len(NTYPE), CH)), S.REGULAR((5,)),
        ],
        compiler_params=pltpu.CompilerParams(collective_id=0, has_side_effects=True, vmem_limit_bytes=67043328) if COMM
        else pltpu.CompilerParams(vmem_limit_bytes=67043328),
        cost_estimate=pl.CostEstimate(flops=6 * 2 * N * D * F, bytes_accessed=200 * 2**20, transcendentals=N * F),
        name="mlp_bwd",
    )(dy, gate, up, wg, wu, wd, x)


def solution(mesh):
    def step(x, dy, gate, up, w_gate, w_up, w_down):
        dx, dwg, dwu, dwd, *_ = call(dy, gate, up, w_gate, w_up, w_down, x)
        return dx, dwg, dwu, dwd

    tokens, columns, rows = P("dp", None), P(None, "tp"), P("tp", None)
    return jax.shard_map(
        step,
        mesh=mesh,
        in_specs=(tokens, tokens, P("dp", "tp"), P("dp", "tp"), columns, columns, rows),
        out_specs=(tokens, P("dp", "tp"), P("dp", "tp"), P(("dp", "tp"), None)),
        check_vma=False,
    )
```

time: 463 us -> 277 us (0.60)
  Pallas kernels: 0 us -> 232 us
  waiting for transfers between devices: 208 us -> 0 us
  matrix products: 195 us -> 0 us
  between operations: 14 us -> 0.64 us
    pallas_call x0 -> x1, Pallas kernels: none -> 232 us  [call(): pl.pallas_call(kernel, in_specs=[any_] * 7, out_specs=[any_] * 7, out_sha...]
    psum x1 -> x0, waiting for transfers between devices: 208 us -> none  [step(): dx = lax.psum(term.astype(jnp.bfloat16), 'tp')]
    dot_general x6 -> x0, matrix products: 195 us -> none  [the longest x1 36.8 us: step(): jnp.dot(d_up, w_up.T, preferred_element_type=jnp.float32)]
    unnamed x3 -> x4, local copies, waits for them, and re-layouts: 46.1 us -> 44.7 us
  transfers between devices with their start and end apart: 1 -> 0, of which waited for: 1 -> 0; matrix products, arithmetic and copies ran while one was open for 27% -> 0% of each run, Pallas kernels for 0% -> 0%
where the time goes in v1:
time: 277 us
  Pallas kernels  232 us (84%)
  local copies, waits for them, and re-layouts  44.7 us (16%)
    pallas_call x1, Pallas kernels, call(): pl.pallas_call(kernel, in_specs=[any_] * 7, out_specs=[any_] * 7, out_sha...  232 us
    unnamed x4, local copies, waits for them, and re-layouts  44.7 us

profile of v1, /device:TPU:0, one launch (start us, length us, event | category | flops | bytes accessed | tf_op | source)
XLA Modules:
  0.0 277.0 jit_solution(18163573946946307964)
XLA Ops:
  0.6 231.7 %mlp_bwd.1 = (bf16[2048,5120]{1,0:T(8,128)(2,1)}, bf16[5120,1024]{1,0:T(8,128)(2,1)}, bf16[5120,1024]{1,0:T(8,128)(2,1)}, bf16[1024,5120]{1,0:T(8,128)(2,1)}, bf...) custom-call(bf16[2048,5120]{1,0:T(8,128)(2,1)} %dy.1, bf16[2048,1024]{1,0:T(8,128)(2,1)} %gate.1, ...), custom_call_target="tpu_custom_call" | custom-call | flops 128849018880 | bytes 209715200 | tf_op jit(solution)/shard_map/mlp_bwd/pallas_call | solution.py:489
  232.3 17.3 %copy.15 = bf16[2048,5120]{1,0:T(8,128)(2,1)} copy(bf16[2048,5120]{1,0:T(8,128)(2,1)} %get-tuple-element.16) | data formatting | bytes 41943040
  249.6 9.3 %copy.16 = bf16[5120,1024]{1,0:T(8,128)(2,1)} copy(bf16[5120,1024]{1,0:T(8,128)(2,1)} %get-tuple-element.17) | data formatting | bytes 20971520
  258.9 9.3 %copy.17 = bf16[5120,1024]{1,0:T(8,128)(2,1)} copy(bf16[5120,1024]{1,0:T(8,128)(2,1)} %get-tuple-element.18) | data formatting | bytes 20971520
  268.2 8.8 %copy.18 = bf16[1024,5120]{1,0:T(8,128)(2,1)} copy(bf16[1024,5120]{1,0:T(8,128)(2,1)} %get-tuple-element.19) | data formatting | bytes 20971520

commit v2 on v1

v2 whole, which is shorter than its diff:
```python
import jax
import jax.numpy as jnp
from jax import lax
from jax.experimental import pallas as pl
from jax.experimental.pallas import tpu as pltpu
from jax.sharding import PartitionSpec as P

N = 2048
D = 5120
F = 1024
R = 256
NT = N // R
RC = 128
CH = N // RC
H, Q, E = RC // 2, RC // 4, RC // 8
TB = 512
NB = D // TB
PT = 6
DEP = 4
KD = 12
CB = 5120
FAKE = False
DOWN2 = False
FS = ()
NOEW = False
BF = jnp.bfloat16
F32 = jnp.float32
COMM = True
COMP = True
OFF = dict(p1=(7, 7), s1=(10, 12), s2=(13, 15), s3=(17, 18), s4=(23, 24), s5=(26, 31), a1=(30, 35), a2=(36, 39), a3=(45, 49), a4=(56, 56))
NTYPE = ("core", "p1", "s1", "s2", "s3", "p3", "a1", "a2", "a3", "ap1", "acore")


def tb_dot(a, b):
    return lax.dot_general(a, b, (((1,), (1,)), ((), ())), preferred_element_type=F32)


def ta_dot(a, b):
    return lax.dot_general(a, b, (((0,), (0,)), ((), ())), preferred_element_type=F32)


def kernel(dy, gate, up, wg, wu, wd, x,
           dx, dwg, dwu, dwd, dgo, duo, hio,
           wdv, wgv, wuv, dyb, gb, ub, dgb, dub, hib,
           own, sb0, sb1, k1, b1, b2, b3, b4, fin,
           lc, lp, l1, l2, l3, l4,
           insem, wsem, osem, bsem, bout, finsem, ss, rs, cred):
    me = lax.axis_index("tp")
    core = lax.rem(me, 2)
    z = lax.rem(me // 2, 4)
    yy = lax.rem(me // 8, 2)
    xx = me // 16
    c0 = core == 0
    inner = jnp.logical_or(z == 1, z == 2)
    outer = jnp.logical_not(inner)
    peer = me + 1 - 2 * core
    xp = me + 16 - 32 * xx
    yp = me + 8 - 16 * yy
    bit1 = jnp.where(c0, xx, yy)
    d1 = jnp.where(c0, xp, yp)
    d3 = jnp.where(c0, yp, xp)
    dz = jnp.where(lax.rem(z, 2) == 0, me + 2, me - 2)
    dm = jnp.where(z == 1, me + 2, me - 2)
    kc = core * H
    kp = bit1 * Q
    sp = (1 - bit1) * Q
    nr = jnp.where(z <= 1, 0, E)
    fr = E - nr
    T = {n: i for i, n in enumerate(NTYPE)}

    class Dummy:
        def start(self): pass
        wait_send = wait_recv = wait = start

    def rd(n, c, src, dst, dev):
        if FAKE or n in FS:
            return Dummy()
        return pltpu.make_async_remote_copy(
            src_ref=src, dst_ref=dst, send_sem=ss.at[T[n], c], recv_sem=rs.at[T[n], c],
            device_id={"tp": dev}, device_id_type=pl.DeviceIdType.MESH)

    def rows(c, off, n):
        return dx.at[pl.ds(pl.multiple_of(c * RC + off, 16), n)]

    def m(c, k=DEP):
        return lax.rem(c, k)

    def cp(n, c):
        s = m(c)
        near, far, both = (rows(c, kc + kp + nr, E), rows(c, kc + kp + fr, E), rows(c, kc + kp, Q))
        if n == "core":
            return rd(n, c, sb0.at[m(c, 2)], lc.at[s], peer)
        if n == "p1":
            return rd(n, c, sb1.at[s], lp.at[s], d1)
        if n == "s1":
            return rd(n, c, b1.at[s], l1.at[s], dz)
        if n == "s2":
            return rd(n, c, b2.at[s], l2.at[s], dm)
        if n == "s3":
            return rd(n, c, b3.at[s], l3.at[s], dz)
        if n == "p3":
            return rd(n, c, b4.at[s], l4.at[s], d3)
        if n == "a1":
            return rd(n, c, fin.at[s], near, dz)
        if n == "a2":
            return rd(n, c, near, near, dm)
        if n == "a3":
            return rd(n, c, far, far, dz)
        if n == "ap1":
            return rd(n, c, both, both, d1)
        return rd(n, c, rows(c, kc, H), rows(c, kc, H), peer)

    def cp_fin(c):
        s = m(c)
        return pltpu.make_async_copy(fin.at[s], rows(c, kc + kp + nr, E), finsem.at[s])

    def recv_a(n, c):
        near, far = rows(c, kc + kp + nr, E), rows(c, kc + kp + fr, E)
        r = {"a1": near, "a2": far, "a3": far}[n]
        rd(n, c, r, r, peer).wait_recv()

    CI = {"core": 0, "p1": 1, "s1": 2, "s2": 3, "s3": 4, "p3": 5}

    def take(n, c):
        if FAKE or n in FS:
            return
        @pl.when(c >= DEP)
        def _():
            pl.semaphore_wait(cred.at[CI[n]], 1)

    def give(n, c, dev):
        if FAKE or n in FS:
            return
        @pl.when(c < CH - DEP)
        def _():
            pl.semaphore_signal(cred.at[CI[n]], inc=1, device_id={"tp": dev}, device_id_type=pl.DeviceIdType.MESH)

    def free(n, c):
        @pl.when(c >= DEP)
        def _():
            cp(n, c - DEP).wait_send()


    def cols(f):
        if NOEW:
            return
        @pl.loop(0, D // CB)
        def _(j):
            f(pl.ds(pl.multiple_of(j * CB, 128), CB))

    def ds_(o, n):
        return pl.ds(pl.multiple_of(o, 16), n)

    def f32(v):
        return v.astype(F32)

    def e_send_core(c):
        take("core", c)
        cp("core", c).start()

    def e_p1(c):
        cp("core", c).wait_send()
        cp("core", c).wait_recv()
        s, t, o = m(c), m(c, KD), m(c, 2)
        free("p1", c)
        take("p1", c)

        def f(cs):
            sb1[s, :, cs] = (own[o, ds_(sp, Q), cs] + f32(lc[s, ds_(sp, Q), cs])).astype(BF)
        cols(f)
        cp("p1", c).start()

        def g(cs):
            k1[t, :, cs] = own[o, ds_(kp, Q), cs] + f32(lc[s, ds_(kp, Q), cs])
        cols(g)
        give("core", c, peer)

    def e_s1(c):
        cp("p1", c).wait_recv()
        s, t = m(c), m(c, KD)

        @pl.when(outer)
        def _():
            free("s1", c)
            take("s1", c)

            def f(cs):
                b1[s, :, cs] = (k1[t, ds_(fr, E), cs] + f32(lp[s, ds_(fr, E), cs])).astype(BF)
            cols(f)
            cp("s1", c).start()

            def g(cs):
                k1[t, ds_(nr, E), cs] = k1[t, ds_(nr, E), cs] + f32(lp[s, ds_(nr, E), cs])
            cols(g)

        @pl.when(inner)
        def _():
            def f(cs):
                k1[t, :, cs] = k1[t, :, cs] + f32(lp[s, :, cs])
            cols(f)

        give("p1", c, d1)

    def hop(n_in, n_out, c, role, half, land, buf, giver):
        @pl.when(role)
        def _():
            cp(n_in, c).wait_recv()
            s, t = m(c), m(c, KD)
            free(n_out, c)
            take(n_out, c)

            def f(cs):
                buf[s, :, cs] = (k1[t, ds_(half, E), cs] + f32(land[s, :, cs])).astype(BF)
            cols(f)
            cp(n_out, c).start()
            give(n_in, c, giver)

    def e_s2(c):
        hop("s1", "s2", c, inner, fr, l1, b2, dz)

    def e_s3(c):
        hop("s2", "s3", c, inner, nr, l2, b3, dm)

    def e_s4(c):
        hop("s3", "p3", c, outer, nr, l3, b4, dz)

    def e_s5(c):
        @pl.when(outer)
        def _():
            cp("p3", c).wait_recv()
            s = m(c)
            free("a1", c)

            def f(cs):
                fin[s, :, cs] = (f32(b4[s, :, cs]) + f32(l4[s, :, cs])).astype(BF)
            cols(f)
            cp("a1", c).start()
            cp_fin(c).start()
            give("p3", c, d3)

    def e_a1(c):
        @pl.when(inner)
        def _():
            recv_a("a1", c)
            cp("a2", c).start()

        @pl.when(outer)
        def _():
            cp_fin(c).wait()

    def e_a2(c):
        @pl.when(inner)
        def _():
            recv_a("a2", c)
            cp("a3", c).start()
            cp("ap1", c).start()

    def e_a3(c):
        @pl.when(outer)
        def _():
            recv_a("a3", c)
            cp("ap1", c).start()

    def e_a4(c):
        cp("ap1", c).wait_recv()
        cp("acore", c).start()

    EV = dict(p1=e_p1, s1=e_s1, s2=e_s2, s3=e_s3, s4=e_s4, s5=e_s5, a1=e_a1, a2=e_a2, a3=e_a3, a4=e_a4)

    def events(t, pos, lo, hi):
        if not COMM:
            return
        for n, offs in OFF.items():
            for odd, off in enumerate(offs):
                dt, ps = divmod(off, PT)
                if ps != pos or hi - 1 - dt < 0 or lo - dt >= NT:
                    continue
                i = t - dt

                @pl.when(jnp.logical_and(i >= 0, i < NT))
                def _(n=n, i=i, odd=odd):
                    EV[n](2 * i + odd)

    if COMM:
        bar = pltpu.get_barrier_semaphore()
        for dev in (peer, d1, dz, jnp.where(inner, dm, d3)):
            pl.semaphore_signal(bar, inc=1, device_id={"tp": dev}, device_id_type=pl.DeviceIdType.MESH)

    def ld_dy(i):
        return pltpu.make_async_copy(dy.at[pl.ds(pl.multiple_of(i * R, R), R)], dyb, insem.at[0])

    def ld_g(i):
        return pltpu.make_async_copy(gate.at[pl.ds(pl.multiple_of(i * R, R), R)], gb, insem.at[1])

    def ld_u(i):
        return pltpu.make_async_copy(up.at[pl.ds(pl.multiple_of(i * R, R), R)], ub, insem.at[2])

    def st(i, k):
        src, dst = ((dgb, dgo), (dub, duo), (hib, hio))[k]
        return pltpu.make_async_copy(src, dst.at[pl.ds(pl.multiple_of(i * R, R), R)], osem.at[k])

    lw = [pltpu.make_async_copy(wd, wdv, wsem.at[0]), pltpu.make_async_copy(wg, wgv, wsem.at[1]), pltpu.make_async_copy(wu, wuv, wsem.at[2])]
    ld_dy(0).start()
    lw[0].start()
    ld_g(0).start()
    ld_u(0).start()
    lw[1].start()
    lw[2].start()
    if COMM:
        pl.semaphore_wait(bar, 4)

    def phase_a(i, _):
        @pl.when(i > 0)
        def _():
            for k in range(3):
                st(i - 1, k).wait()

        @pl.when(i == 0)
        def _():
            lw[0].wait()
        ld_dy(i).wait()
        ld_g(i).wait()
        ld_u(i).wait()

        def dblock(j):
            cs = pl.ds(j * 512, 512)
            dh = tb_dot(dyb[...], wdv[cs, :]) if COMP else dyb[:, 0:512].astype(F32)
            g = gb[:, cs].astype(F32)
            u = ub[:, cs].astype(F32)
            s = 1.0 / (1.0 + jnp.exp(-g))
            gs = g * s
            dgb[:, cs] = (dh * u * (s + gs * (1.0 - s))).astype(BF)
            dub[:, cs] = (dh * gs).astype(BF)
            hib[:, cs] = (gs * u).astype(BF)

        dblock(0)
        events(i, 0, 0, NT)
        dblock(1)
        for k in range(3):
            st(i, k).start()

        @pl.when(i < NT - 1)
        def _():
            ld_dy(i + 1).start()
            ld_g(i + 1).start()
            ld_u(i + 1).start()

        events(i, 1, 0, NT)

        @pl.when(i == 0)
        def _():
            lw[1].wait()
            lw[2].wait()

        def tblock(j):
            rs_ = pl.ds(pl.multiple_of(j * 512, 512), 512)
            t = tb_dot(dgb[...], wgv[rs_, :]) + tb_dot(dub[...], wuv[rs_, :]) if COMP else dyb[:, rs_].astype(F32)
            for o in range(2):
                a, b = t[2 * o * H:(2 * o + 1) * H], t[(2 * o + 1) * H:(2 * o + 2) * H]
                own[o, :, rs_] = jnp.where(c0, a, b)
                sb0[o, :, rs_] = jnp.where(c0, b, a).astype(BF)

        for p, (lo, hi) in enumerate(((0, 3), (3, 5), (5, 8), (8, 10))):
            pl.loop(lo, hi)(tblock)
            if p == 3 and COMM:
                e_send_core(2 * i)
                e_send_core(2 * i + 1)
            events(i, 2 + p, 0, NT)
        return 0

    lax.fori_loop(0, NT, phase_a, 0)
    for k in range(3):
        st(NT - 1, k).wait()

    dgv, duv = wgv.at[pl.ds(0, N)], wgv.at[pl.ds(N, N)]
    hiv = wuv.at[pl.ds(0, N)]
    K2 = N // 2

    def ld_x(b):
        s = lax.rem(b, 2)
        return pltpu.make_async_copy(x.at[:, pl.ds(pl.multiple_of(b * TB, TB), TB)],
                                     wuv.at[pl.ds(N, N), pl.ds(pl.multiple_of(s * TB, TB), TB)], bsem.at[0, s])

    def ld_dyc(b, h):
        s = lax.rem(b, 2)
        return pltpu.make_async_copy(dy.at[pl.ds(h * K2, K2), pl.ds(pl.multiple_of(b * TB, TB), TB)],
                                     wdv.at[:, pl.ds(pl.multiple_of(s * 2 * TB, TB) + h * TB, TB)], bsem.at[1 + h, s])

    def out_g(b, k):
        s = lax.rem(b, 2)
        v = (wgv, wuv)[k]
        return pltpu.make_async_copy(v.at[pl.ds(pl.multiple_of(2 * N + s * TB, TB), TB)],
                                     (dwg, dwu)[k].at[pl.ds(pl.multiple_of(b * TB, TB), TB)], bout.at[k, s])

    def out_d(b):
        s = lax.rem(b, 2)
        return pltpu.make_async_copy(wdv.at[:, pl.ds(pl.multiple_of(4096 + s * TB, TB), TB)],
                                     dwd.at[:, pl.ds(pl.multiple_of(b * TB, TB), TB)], bout.at[2, s])

    lb = [pltpu.make_async_copy(dgo, dgv, wsem.at[0]), pltpu.make_async_copy(duo, duv, wsem.at[1]), pltpu.make_async_copy(hio, hiv, wsem.at[2])]
    lb[0].start()
    ld_x(0).start()
    lb[1].start()
    if not DOWN2:
        lb[2].start()
        ld_dyc(0, 0).start()
        ld_dyc(0, 1).start()

    def phase_b(b, _):
        t = b + NT
        s = lax.rem(b, 2)

        @pl.when(b < NB - 1)
        def _():
            ld_x(b + 1).start()
            if not DOWN2:
                ld_dyc(b + 1, 0).start()
                ld_dyc(b + 1, 1).start()

        @pl.when(b == 0)
        def _():
            lb[0].wait()
        ld_x(b).wait()
        xs = pl.ds(pl.multiple_of(s * TB, TB), TB)
        for k in range(2):
            @pl.when(b >= 2)
            def _():
                out_g(b - 2, k).wait()

            if k == 1:
                @pl.when(b == 0)
                def _():
                    lb[1].wait()
            r = ta_dot(wuv[pl.ds(N, N), xs], (dgv, duv)[k][...]) if COMP else wuv[0:512, :].astype(F32)
            (wgv, wuv)[k][pl.ds(pl.multiple_of(2 * N + s * TB, TB), TB), :] = r.astype(BF)
            out_g(b, k).start()
            events(t, 2 * k, NT, NT + NB)
            events(t, 2 * k + 1, NT, NT + NB)

        if not DOWN2:
            @pl.when(b >= 2)
            def _():
                out_d(b - 2).wait()

            @pl.when(b == 0)
            def _():
                lb[2].wait()
            ld_dyc(b, 0).wait()
            ld_dyc(b, 1).wait()
            y0 = wdv[:, pl.ds(pl.multiple_of(s * 2 * TB, TB), TB)]
            y1 = wdv[:, pl.ds(pl.multiple_of(s * 2 * TB, TB) + TB, TB)]
            r = ta_dot(hiv[pl.ds(0, K2), :], y0) + ta_dot(hiv[pl.ds(K2, K2), :], y1) if COMP else y0.astype(F32)
            wdv[:, pl.ds(pl.multiple_of(4096 + s * TB, TB), TB)] = r.astype(BF)
            out_d(b).start()
        events(t, 4, NT, NT + NB)
        events(t, 5, NT, NT + NB)
        return 0

    lax.fori_loop(0, NB, phase_b, 0)
    last = NT + max(o for v in OFF.values() for o in v) // PT
    if COMM and last > NT + NB:
        def drain(t, _):
            for p in range(PT):
                events(t, p, NT + NB, last)
            return 0
        lax.fori_loop(NT + NB, last, drain, 0)

    for b in (NB - 2, NB - 1):
        out_g(b, 0).wait()
        out_g(b, 1).wait()
        if not DOWN2:
            out_d(b).wait()
    if COMM:
        def tail(c, _):
            cp("acore", c).wait_recv()
            cp("acore", c).wait_send()
            cp("ap1", c).wait_send()

            @pl.when(inner)
            def _():
                cp("a2", c).wait_send()
                cp("a3", c).wait_send()
            return 0
        lax.fori_loop(0, CH, tail, 0)

        def tail2(c, _):
            cp("p1", c).wait_send()

            @pl.when(inner)
            def _():
                cp("s2", c).wait_send()
                cp("s3", c).wait_send()

            @pl.when(outer)
            def _():
                cp("s1", c).wait_send()
                cp("p3", c).wait_send()
                cp("a1", c).wait_send()
            return 0
        lax.fori_loop(CH - DEP, CH, tail2, 0)


def call(dy, gate, up, wg, wu, wd, x):
    s = jax.ShapeDtypeStruct
    V = pltpu.VMEM
    S = pltpu.SemaphoreType
    any_ = pl.BlockSpec(memory_space=pl.ANY)
    return pl.pallas_call(
        kernel,
        in_specs=[any_] * 7,
        out_specs=[any_] * 7,
        out_shape=[s((N, D), BF), s((D, F), BF), s((D, F), BF), s((F, D), BF), s((N, F), BF), s((N, F), BF), s((N, F), BF)],
        scratch_shapes=[
            V((F, D), BF), V((D, F), BF), V((D, F), BF), V((R, D), BF), V((R, F), BF), V((R, F), BF),
            V((R, F), BF), V((R, F), BF), V((R, F), BF),
            V((2, H, D), F32), V((2, H, D), BF), V((DEP, Q, D), BF), V((KD, Q, D), F32),
            V((DEP, E, D), BF), V((DEP, E, D), BF), V((DEP, E, D), BF), V((DEP, E, D), BF), V((DEP, E, D), BF),
            V((DEP, H, D), BF), V((DEP, Q, D), BF), V((DEP, E, D), BF), V((DEP, E, D), BF), V((DEP, E, D), BF), V((DEP, E, D), BF),
            S.DMA((3,)), S.DMA((3,)), S.DMA((3,)), S.DMA((3, 2)), S.DMA((3, 2)), S.DMA((DEP,)),
            S.DMA((len(NTYPE), CH)), S.DMA((len(NTYPE), CH)), S.REGULAR((6,)),
        ],
        compiler_params=pltpu.CompilerParams(collective_id=0, has_side_effects=True, vmem_limit_bytes=67043328) if COMM
        else pltpu.CompilerParams(vmem_limit_bytes=67043328),
        cost_estimate=pl.CostEstimate(flops=6 * 2 * N * D * F, bytes_accessed=200 * 2**20, transcendentals=N * F),
        name="mlp_bwd",
    )(dy, gate, up, wg, wu, wd, x)


def finish_kernel(hi, dy, dx, dwg, dwu, dwd, odx, odwg, odwu, odwd):
    odx[...] = dx[...]
    odwg[...] = dwg[...]
    odwu[...] = dwu[...]
    if DOWN2:
        odwd[...] = ta_dot(hi[...], dy[...]).astype(BF)
    else:
        odwd[...] = dwd[...]


def finish(hi, dy, dx, dwg, dwu, dwd):
    s = jax.ShapeDtypeStruct
    col = lambda n: pl.BlockSpec((n, TB), lambda j: (0, j))
    row = pl.BlockSpec((TB, F), lambda j: (j, 0))
    any_ = pl.BlockSpec(memory_space=pl.ANY)
    return pl.pallas_call(
        finish_kernel,
        grid=(NB,),
        in_specs=[pl.BlockSpec((N, F), lambda j: (0, 0)) if DOWN2 else any_, col(N) if DOWN2 else any_, col(N), row, row, any_ if DOWN2 else col(F)],
        out_specs=[col(N), row, row, col(F)],
        out_shape=[s((N, D), BF), s((D, F), BF), s((D, F), BF), s((F, D), BF)],
        compiler_params=pltpu.CompilerParams(vmem_limit_bytes=60 * 2**20),
        cost_estimate=pl.CostEstimate(flops=2 * N * D * F, bytes_accessed=118 * 2**20, transcendentals=0),
        name="finish",
    )(hi, dy, dx, dwg, dwu, dwd)


def solution(mesh):
    def step(x, dy, gate, up, w_gate, w_up, w_down):
        dx, dwg, dwu, dwd, _, _, hi = call(dy, gate, up, w_gate, w_up, w_down, x)
        return finish(hi, dy, dx, dwg, dwu, dwd)

    tokens, columns, rows = P("dp", None), P(None, "tp"), P("tp", None)
    return jax.shard_map(
        step,
        mesh=mesh,
        in_specs=(tokens, tokens, P("dp", "tp"), P("dp", "tp"), columns, columns, rows),
        out_specs=(tokens, P("dp", "tp"), P("dp", "tp"), P(("dp", "tp"), None)),
        check_vma=False,
    )
```

time: 277 us -> 237 us (0.86)
  local copies, waits for them, and re-layouts: 44.7 us -> 0 us
  Pallas kernels: 232 us -> 236 us
    unnamed x4 -> x0, local copies, waits for them, and re-layouts: 44.7 us -> none
    pallas_call x0 -> x1, Pallas kernels: none -> 33.6 us  [finish(): pl.pallas_call(finish_kernel, grid=(NB,), in_specs=[pl.BlockSpec((N, F),...]
    pallas_call x1, Pallas kernels: 232 us -> 203 us  [call(): pl.pallas_call(kernel, in_specs=[any_] * 7, out_specs=[any_] * 7, out_sha...]
where the time goes in v2:
time: 237 us
  Pallas kernels  236 us (100%)
    pallas_call x1, Pallas kernels, call(): pl.pallas_call(kernel, in_specs=[any_] * 7, out_specs=[any_] * 7, out_sha...  203 us
    pallas_call x1, Pallas kernels, finish(): pl.pallas_call(finish_kernel, grid=(NB,), in_specs=[pl.BlockSpec((N, F),...  33.6 us

profile of v2, /device:TPU:0, one launch (start us, length us, event | category | flops | bytes accessed | tf_op | source)
XLA Modules:
  0.0 237.1 jit_solution(9409048670859449477)
XLA Ops:
  0.6 202.8 %mlp_bwd.1 = (bf16[2048,5120]{1,0:T(8,128)(2,1)}, bf16[5120,1024]{1,0:T(8,128)(2,1)}, bf16[5120,1024]{1,0:T(8,128)(2,1)}, bf16[1024,5120]{1,0:T(8,128)(2,1)}, bf...) custom-call(bf16[2048,5120]{1,0:T(8,128)(2,1)} %dy.3, bf16[2048,1024]{1,0:T(8,128)(2,1)} %gate.1, ...), custom_call_target="tpu_custom_call" | custom-call | flops 128849018880 | bytes 209715200 | tf_op jit(solution)/shard_map/mlp_bwd/pallas_call | solution.py:508
  203.4 33.6 %finish.1 = (bf16[2048,5120]{1,0:T(8,128)(2,1)}, bf16[5120,1024]{1,0:T(8,128)(2,1)}, bf16[5120,1024]{1,0:T(8,128)(2,1)}, bf16[1024,5120]{1,0:T(8,128)(2,1)}) custom-call(bf16[2048,1024]{1,0:T(8,128)(2,1)} %get-tuple-element.9.hi, bf16[2048,5120]{1,0:T(8,128)(2,1)} %dy.3, bf16[2048,5120]{1,0:T(8,128)(2,1)} %get-tuple-element.10.dx, ...), custom_call_target="tpu_custom_call" | custom-call | flops 21474836480 | bytes 123731968 | tf_op jit(solution)/shard_map/finish/pallas_call | solution.py:544

commit v3 on v2

--- a/solution.py
+++ b/solution.py
@@ -299,11 +299,13 @@
         src, dst = ((dgb, dgo), (dub, duo), (hib, hio))[k]
         return pltpu.make_async_copy(src, dst.at[pl.ds(pl.multiple_of(i * R, R), R)], osem.at[k])
 
-    lw = [pltpu.make_async_copy(wd, wdv, wsem.at[0]), pltpu.make_async_copy(wg, wgv, wsem.at[1]), pltpu.make_async_copy(wu, wuv, wsem.at[2])]
+    lwd = [pltpu.make_async_copy(wd.at[pl.ds(k * 512, 512)], wdv.at[pl.ds(k * 512, 512)], wsem.at[(0, 3)[k]]) for k in range(2)]
+    lw = [None, pltpu.make_async_copy(wg, wgv, wsem.at[1]), pltpu.make_async_copy(wu, wuv, wsem.at[2])]
     ld_dy(0).start()
-    lw[0].start()
+    lwd[0].start()
     ld_g(0).start()
     ld_u(0).start()
+    lwd[1].start()
     lw[1].start()
     lw[2].start()
     if COMM:
@@ -317,7 +319,7 @@
 
         @pl.when(i == 0)
         def _():
-            lw[0].wait()
+            lwd[0].wait()
         ld_dy(i).wait()
         ld_g(i).wait()
         ld_u(i).wait()
@@ -335,6 +337,11 @@
 
         dblock(0)
         events(i, 0, 0, NT)
+
+        @pl.when(i == 0)
+        def _():
+            lwd[1].wait()
+
         dblock(1)
         for k in range(3):
             st(i, k).start()
@@ -516,7 +523,7 @@
             V((2, H, D), F32), V((2, H, D), BF), V((DEP, Q, D), BF), V((KD, Q, D), F32),
             V((DEP, E, D), BF), V((DEP, E, D), BF), V((DEP, E, D), BF), V((DEP, E, D), BF), V((DEP, E, D), BF),
             V((DEP, H, D), BF), V((DEP, Q, D), BF), V((DEP, E, D), BF), V((DEP, E, D), BF), V((DEP, E, D), BF), V((DEP, E, D), BF),
-            S.DMA((3,)), S.DMA((3,)), S.DMA((3,)), S.DMA((3, 2)), S.DMA((3, 2)), S.DMA((DEP,)),
+            S.DMA((3,)), S.DMA((4,)), S.DMA((3,)), S.DMA((3, 2)), S.DMA((3, 2)), S.DMA((DEP,)),
             S.DMA((len(NTYPE), CH)), S.DMA((len(NTYPE), CH)), S.REGULAR((6,)),
         ],
         compiler_params=pltpu.CompilerParams(collective_id=0, has_side_effects=True, vmem_limit_bytes=67043328) if COMM

time: 237 us -> 237 us (level)
  no operation moved by 1% of the time
where the time goes in v3:
time: 237 us
  Pallas kernels  236 us (100%)
    pallas_call x1, Pallas kernels, call(): pl.pallas_call(kernel, in_specs=[any_] * 7, out_specs=[any_] * 7, out_sha...  203 us
    pallas_call x1, Pallas kernels, finish(): pl.pallas_call(finish_kernel, grid=(NB,), in_specs=[pl.BlockSpec((N, F),...  33.6 us

profile of v3, /device:TPU:0, one launch (start us, length us, event | category | flops | bytes accessed | tf_op | source)
XLA Modules:
  0.0 237.1 jit_solution(18149395767204103741)
XLA Ops:
  0.6 202.8 %mlp_bwd.1 = (bf16[2048,5120]{1,0:T(8,128)(2,1)}, bf16[5120,1024]{1,0:T(8,128)(2,1)}, bf16[5120,1024]{1,0:T(8,128)(2,1)}, bf16[1024,5120]{1,0:T(8,128)(2,1)}, bf...) custom-call(bf16[2048,5120]{1,0:T(8,128)(2,1)} %dy.3, bf16[2048,1024]{1,0:T(8,128)(2,1)} %gate.1, ...), custom_call_target="tpu_custom_call" | custom-call | flops 128849018880 | bytes 209715200 | tf_op jit(solution)/shard_map/mlp_bwd/pallas_call | solution.py:515
  203.4 33.6 %finish.1 = (bf16[2048,5120]{1,0:T(8,128)(2,1)}, bf16[5120,1024]{1,0:T(8,128)(2,1)}, bf16[5120,1024]{1,0:T(8,128)(2,1)}, bf16[1024,5120]{1,0:T(8,128)(2,1)}) custom-call(bf16[2048,1024]{1,0:T(8,128)(2,1)} %get-tuple-element.9.hi, bf16[2048,5120]{1,0:T(8,128)(2,1)} %dy.3, bf16[2048,5120]{1,0:T(8,128)(2,1)} %get-tuple-element.10.dx, ...), custom_call_target="tpu_custom_call" | custom-call | flops 21474836480 | bytes 123731968 | tf_op jit(solution)/shard_map/finish/pallas_call | solution.py:551
